TPU v7x, 32 devices: a whole 2x2x4 slice. The times are simulated.
32 devices in a mesh: member: 2 (over y), tile: 4 (over z), row: 2 (over x), lev: 2 (over core).
Axes of the slice: x: 2, y: 2, z: 4, core: 2. Of those that a mesh axis runs over, the one named last changes fastest.
Arguments:
- thickness: float32 [128, 64, 256], P(('member', 'lev'), 'tile', 'row'), parts along dimension 0, may hold values from 0.24 to 14.91
- zonal_wind: float32 [128, 64, 256], P(('member', 'lev'), 'tile', 'row'), parts along dimension 0, may hold values from -1.8 to 1.8
- merid_wind: float32 [128, 64, 256], P(('member', 'lev'), 'tile', 'row'), parts along dimension 0, may hold values from -1.8 to 1.8
- pert_codes: int32 [128, 256], P(('member', 'tile'), 'row'), parts along dimension 0, may hold values from 0 to 1073741823
Outputs:
- thick_out: float32 [128, 64, 256], P(('member', 'lev'), 'tile', 'row'), parts along dimension 0
- zonal_out: float32 [128, 64, 256], P(('member', 'lev'), 'tile', 'row'), parts along dimension 0
- merid_out: float32 [128, 64, 256], P(('member', 'lev'), 'tile', 'row'), parts along dimension 0
There are 2 independent parts, one for each index of `member`. A program takes and returns all parts, laid end to end along the dimension named above; each array names one. Nothing has to cross between parts.
All inputs are finite; a program needn't handle non-finite values.
Results may differ from a plain program's by a relative error of at most 0.0003.
Values sent between devices are 32-bit elements; how exact they have to be, the bound alone decides.
A program may use at most 64 MiB of HBM per device.

v0:
```python
import jax
import jax.numpy as jnp
from jax import lax
from jax.sharding import PartitionSpec as P

NSUB = 4


CFL_NUMBER = 0.8


def padded(block, sides, width):
    for axis, dim in sides:
        count = lax.axis_size(axis)
        forward = [(i, i + 1) for i in range(count - 1)]
        forward.append((count - 1, 0))
        backward = [(target, source) for source, target in forward]
        low = lax.ppermute(
            lax.slice_in_dim(block, block.shape[dim] - width, None, axis=dim), axis, forward
        )
        high = lax.ppermute(lax.slice_in_dim(block, 0, width, axis=dim), axis, backward)
        block = jnp.concatenate([low, block, high], axis=dim)
    return block


def advance(stacked, half_step):
    height = stacked[0]
    zonal = stacked[1]
    merid = stacked[2]
    zonal_new = zonal[:, 1:-1, 1:-1] - half_step * (height[:, 2:, 1:-1] - height[:, :-2, 1:-1])
    merid_new = merid[:, 1:-1, 1:-1] - half_step * (height[:, 1:-1, 2:] - height[:, 1:-1, :-2])
    centre = height[:, 1:-1, 1:-1]
    flux_east = centre * zonal_new
    flux_north = centre * merid_new
    height_new = centre[:, 1:-1, 1:-1] - half_step * (
        flux_east[:, 2:, 1:-1]
        - flux_east[:, :-2, 1:-1]
        + (flux_north[:, 1:-1, 2:] - flux_north[:, 1:-1, :-2])
    )
    return jnp.stack([height_new, zonal_new[:, 1:-1, 1:-1], merid_new[:, 1:-1, 1:-1]])


def remap_columns(columns, first, count):
    height = columns[0]
    zonal = columns[1]
    merid = columns[2]
    levels = height.shape[0]
    total = jnp.sum(height, 0)
    tops = jnp.cumsum(height, 0) - height
    marks = (first + jnp.arange(count + 1)).astype(jnp.float32)
    targets = total[None] * (marks / levels)[:, None, None]
    zonal_sum = jnp.zeros(targets.shape, jnp.float32)
    merid_sum = jnp.zeros(targets.shape, jnp.float32)
    for block in range(levels // 8):
        lower = block * 8
        upper = lower + 8
        over = jnp.clip(targets[None] - tops[lower:upper, None], 0.0, height[lower:upper, None])
        zonal_sum = zonal_sum + jnp.sum(zonal[lower:upper, None] * over, 0)
        merid_sum = merid_sum + jnp.sum(merid[lower:upper, None] * over, 0)
    layer = total / levels
    thick_new = jnp.broadcast_to(layer, (count,) + layer.shape)
    zonal_new = (zonal_sum[1:] - zonal_sum[:-1]) / layer
    merid_new = (merid_sum[1:] - merid_sum[:-1]) / layer
    return jnp.stack([thick_new, zonal_new, merid_new])


def local(thickness, zonal_wind, merid_wind, pert_codes):
    bump = 2.0 * (pert_codes % 4096).astype(jnp.float32) / 4095.0
    raised = thickness + bump[None]
    local_peak = jnp.max(raised)
    base_mass = jnp.sum(thickness)
    raised_mass = jnp.sum(raised)
    peak = lax.pmax(local_peak, ("tile", "row", "lev"))
    base_total, raised_total = lax.psum((base_mass, raised_mass), ("tile", "row", "lev"))
    height = raised * (base_total / raised_total)
    half_step = 0.5 * CFL_NUMBER / jnp.sqrt(peak)
    state = jnp.stack([height, zonal_wind, merid_wind])
    state = padded(state, (("tile", 2), ("row", 3)), 2 * NSUB)
    for substep in range(NSUB):
        state = advance(state, half_step)
    levels_here = state.shape[1]
    columns = lax.all_gather(state, "lev", axis=1, tiled=True)
    result = remap_columns(columns, lax.axis_index("lev") * levels_here, levels_here)
    return (result[0], result[1], result[2])


def solution(mesh):
    in_specs = (
        P(("member", "lev"), "tile", "row"),
        P(("member", "lev"), "tile", "row"),
        P(("member", "lev"), "tile", "row"),
        P(("member", "tile"), "row"),
    )
    out_specs = (
        P(("member", "lev"), "tile", "row"),
        P(("member", "lev"), "tile", "row"),
        P(("member", "lev"), "tile", "row"),
    )
    return jax.shard_map(local, mesh=mesh, in_specs=in_specs, out_specs=out_specs, check_vma=False)
```

profile of v0, /device:TPU:0, one launch (start us, length us, event | category | flops | bytes accessed | tf_op | source)
XLA Modules:
  0.0 147.5 jit_solution(1261217638161995393)
XLA Ops:
  7.2 0.8 fusion.38
  8.0 1.6 %add_reduce_fusion = (f32[]{:T(128)}, f32[]{:T(128)}, f32[]{:T(128)}) fusion(f32[32,16,128]{2,1,0:T(8,128)} %param.4, f32[16,128]{1,0:T(8,128)S(1)} %fusion.38), kind=kLoop, calls=%fused_computation.98 | loop fusion | flops 262141 | bytes 270348 | tf_op jit(solution)/shard_map/reduce_max | solution.py:70
  9.6 35.6 %all-reduce = (f32[]{:T(128)}, f32[]{:T(128)}) all-reduce(f32[]{:T(128)} %get-tuple-element.33, f32[]{:T(128)} %get-tuple-element.32), channel_id=1, replica_groups=mesh['member'=2,'tile'=4,'row'=2,'lev'=2] {'tile','row','lev'}, use_global_device_ids=true, to_apply=%region_1.2 | all-reduce | flops 2 | bytes 16 | tf_op jit(solution)/shard_map/psum | solution.py:74
  46.6 1.0 multiply_bitcast_fusion
  47.6 1.1 pad_maximum_fusion.2
  48.8 3.8 %collective-permute-start.1 = (f32[3,32,8,128]{3,2,1,0:T(8,128)S(1)}, f32[3,32,8,128]{3,2,1,0:T(8,128)S(1)}, u32[]{:S(2)}, u32[]{:S(2)}) collective-permute-start(f32[3,32,8,128]{3,2,1,0:T(8,128)S(1)} %get-tuple-element.90), channel_id=1, source_target_pairs={{4,0},{8,4},{12,8},{0,12},{5,1},{9,5},{13,9},{1,13},{6,2},{10,6},{... | collective-permute-start | bytes 1179656 | tf_op jit(solution)/shard_map/ppermute | solution.py:21
  52.6 9.4 %collective-permute-done = f32[3,32,8,128]{3,2,1,0:T(8,128)S(1)} collective-permute-done((f32[3,32,8,128]{3,2,1,0:T(8,128)S(1)}, f32[3,32,8,128]{3,2,1,0:T(8,128)S(1)}, u32[]{:S(2)}, u32[]{:S(2)}) %collective-permute-start) | collective-permute-done | bytes 393248 | tf_op jit(solution)/shard_map/ppermute | solution.py:18
  62.0 2.3 %collective-permute-done.1 = f32[3,32,8,128]{3,2,1,0:T(8,128)S(1)} collective-permute-done((f32[3,32,8,128]{3,2,1,0:T(8,128)S(1)}, f32[3,32,8,128]{3,2,1,0:T(8,128)S(1)}, u32[]{:S(2)}, u32[]{:S(2)}) %collective-permute-start.1) | collective-permute-done | bytes 393248 | tf_op jit(solution)/shard_map/ppermute | solution.py:21
  64.3 0.7 copy-done.4
  65.2 0.6 fusion.47
  65.8 1.2 copy.11
  67.0 0.5 copy.12
  67.5 2.1 %collective-permute-start.3 = (f32[3,32,32,8]{2,3,1,0:T(8,128)S(1)}, f32[3,32,32,8]{2,3,1,0:T(8,128)}, u32[]{:S(2)}, u32[]{:S(2)}) collective-permute-start(f32[3,32,32,8]{2,3,1,0:T(8,128)S(1)} %copy.12), channel_id=1, source_target_pairs={{2,0},{0,2},{3,1},{1,3},{6,4},{4,6},{7,5},{5,7},{10,8},{8,10},{11,... | collective-permute-start | bytes 294920 | tf_op jit(solution)/shard_map/ppermute | solution.py:21
  69.5 38.0 %pmax.7 = f32[]{:T(128)} all-reduce(f32[]{:T(128)} %get-tuple-element.31), channel_id=1, replica_groups=mesh['member'=2,'tile'=4,'row'=2,'lev'=2] {'tile','row','lev'}, use_global_device_ids=true, to_apply=%region_5.6 | all-reduce | flops 1 | bytes 8 | tf_op jit(solution)/shard_map/pmax | solution.py:73
  108.3 0.5 copy.13
  108.8 1.5 %copy.14 = f32[3,32,32,8]{3,2,1,0:T(8,128)S(1)} copy(f32[3,32,32,8]{2,3,1,0:T(8,128)} %collective-permute-done.3) | data formatting | bytes 196608 | tf_op jit(solution)/shard_map/ppermute | solution.py:21
  110.3 2.6 %pad_maximum_fusion = f32[3,32,32,144]{3,2,1,0:T(8,128)S(1)} fusion(f32[3,32,32,8]{3,2,1,0:T(8,128)S(1)} %copy.14, f32[3,32,8,128]{3,2,1,0:T(8,128)} %copy-done.4, f32[1,32,16,128]{3,2,1,0:T(8,128)} %bitcast.71, f32[1,32,16,128]{3,2,1,0:T(8,128)} %bitcast.74, f32[1,32,16,128]{3,2,1,0:T(8,128)S(1)} %multiply_bitcast_fusion, f32[3,32,8,128]{3,2,1,0:T(8,128)} %copy-done.3, ...), kind=kLoop, calls=%fused_computation | loop fusion | flops 2654208 | bytes 3538944 | tf_op jit(solution)/shard_map/concatenate | solution.py:22
  113.2 1.7 %slice_multiply_fusion.3 = (f32[32,30,142]{2,1,0:T(8,128)S(1)}, f32[32,30,142]{2,1,0:T(8,128)S(1)}, f32[32,30,142]{2,1,0:T(8,128)S(1)}, f32[32,30,142]{2,1,0:T(8,128)S(1)}) fusion(f32[32,32,144]{2,1,0:T(8,128)S(1)} %get-tuple-element.54, f32[]{:T(128)S(6)} %div.39, f32[32,32,144]{2,1,0:T(8,128)S(1)} %get-tuple-element.52, ...), kind=kLoop, calls=%fused_computation.49 | loop fusion | flops 1090560 | bytes 5998084 | tf_op jit(solution)/shard_map/mul | solution.py:33
  114.9 1.2 fusion.6
  116.1 1.7 %slice_multiply_fusion.1 = (f32[32,26,138]{2,1,0:T(8,128)S(1)}, f32[32,26,138]{2,1,0:T(8,128)S(1)}, f32[32,26,138]{2,1,0:T(8,128)S(1)}, f32[32,26,138]{2,1,0:T(8,128)S(1)}) fusion(f32[32,28,140]{2,1,0:T(8,128)S(1)} %fusion.6, f32[]{:T(128)S(6)} %div.39, f32[32,30,142]{2,1,0:T(8,128)S(1)} %get-tuple-element.49, f32[32,30,142]{2,1,0:T(8,128)S(1)} %get-tuple-element.84), kind=kLoop, calls=%fused_computation.47 | loop fusion | flops 918528 | bytes 5051908 | tf_op jit(solution)/shard_map/mul | solution.py:33
  117.8 0.9 fusion.24
  118.7 1.3 slice_multiply_fusion.7
  120.0 0.9 fusion.17
  120.9 1.3 slice_multiply_fusion.5
  122.2 0.4 fusion.35
  122.8 0.9 pad_maximum_fusion.3
  123.8 7.2 %all-gather.2.cloned.1.call-done = f32[3,64,16,128]{3,2,1,0:T(8,128)} async-done(((f32[3,32,16,128]{3,2,1,0:T(8,128)}), f32[3,64,16,128]{3,2,1,0:T(8,128)}) %all-gather.2.cloned.1.call-update) | async-done | bytes 1572880 | tf_op jit(solution)/shard_map/all_gather | solution.py:82
  131.0 1.4 bitcast_subtract_fusion
  133.1 2.9 %multiply_reduce_fusion.7 = (f32[33,16,128]{2,1,0:T(8,128)S(1)}, f32[33,16,128]{2,1,0:T(8,128)S(1)}, f32[33,16,128]{2,1,0:T(8,128)S(1)}, f32[33,16,128]{2,1,0:T(...) fusion(f32[8,16,128]{2,1,0:T(8,128)S(1)} %get-tuple-element.62,, ...), kind=kLoop, calls=%fused_computation.8 | loop fusion | flops 14598144 | bytes 3481600 | tf_op jit(solution)/shard_map/reduce_sum | solution.py:59
  136.0 2.7 %multiply_reduce_fusion.6 = (f32[33,16,128]{2,1,0:T(8,128)S(1)}, f32[33,16,128]{2,1,0:T(8,128)S(1)}, f32[33,16,128]{2,1,0:T(8,128)S(1)}, f32[33,16,128]{2,1,0:T(...) fusion(f32[8,16,128]{2,1,0:T(8,128)S(1)} %get-tuple-element.61,, ...), kind=kLoop, calls=%fused_computation.7 | loop fusion | flops 14598144 | bytes 3481600 | tf_op jit(solution)/shard_map/reduce_sum | solution.py:59
  139.1 0.9 fusion.30
  139.9 0.7 squeeze.20
  (28 shorter events, 1.9 us)
Async XLA Ops:
  7.2 57.9 %copy-start.2 = (f32[32,16,128]{2,1,0:T(8,128)S(1)}, f32[32,16,128]{2,1,0:T(8,128)}, u32[]{:S(2)}) copy-start(f32[32,16,128]{2,1,0:T(8,128)} %param.5) | copy-start | bytes 786436
  7.2 57.9 %copy-start.1 = (f32[32,16,128]{2,1,0:T(8,128)S(1)}, f32[32,16,128]{2,1,0:T(8,128)}, u32[]{:S(2)}) copy-start(f32[32,16,128]{2,1,0:T(8,128)} %param.6) | copy-start | bytes 786436
  7.2 123.8 %all-gather.2.cloned.1.call-start = ((), (), s32[]{:S(2)}) async-start(), calls=%async_computation | async-start | bytes 2359296 | tf_op jit(solution)/shard_map/all_gather | solution.py:82
  48.7 13.2 %collective-permute-start = (f32[3,32,8,128]{3,2,1,0:T(8,128)S(1)}, f32[3,32,8,128]{3,2,1,0:T(8,128)S(1)}, u32[]{:S(2)}, u32[]{:S(2)}) collective-permute-start(f32[3,32,8,128]{3,2,1,0:T(8,128)S(1)} %get-tuple-element.89), channel_id=1, source_target_pairs={{0,4},{4,8},{8,12},{12,0},{1,5},{5,9},{9,13},{13,1},{2,6},{6,10},{... | collective-permute-start | bytes 1179656 | tf_op jit(solution)/shard_map/ppermute | solution.py:18
  48.8 15.5 %collective-permute-start.1 = (f32[3,32,8,128]{3,2,1,0:T(8,128)S(1)}, f32[3,32,8,128]{3,2,1,0:T(8,128)S(1)}, u32[]{:S(2)}, u32[]{:S(2)}) collective-permute-start(f32[3,32,8,128]{3,2,1,0:T(8,128)S(1)} %get-tuple-element.90), channel_id=1, source_target_pairs={{4,0},{8,4},{12,8},{0,12},{5,1},{9,5},{13,9},{1,13},{6,2},{10,6},{... | collective-permute-start | bytes 1179656 | tf_op jit(solution)/shard_map/ppermute | solution.py:21
  62.0 2.3 %copy-start.3 = (f32[3,32,8,128]{3,2,1,0:T(8,128)}, f32[3,32,8,128]{3,2,1,0:T(8,128)S(1)}, u32[]{:S(2)}) copy-start(f32[3,32,8,128]{3,2,1,0:T(8,128)S(1)} %collective-permute-done) | copy-start | bytes 1179652
  64.3 0.7 copy-start.4
  67.0 41.3 %collective-permute-start.2 = (f32[3,32,32,8]{2,3,1,0:T(8,128)}, f32[3,32,32,8]{2,3,1,0:T(8,128)S(1)}, u32[]{:S(2)}, u32[]{:S(2)}) collective-permute-start(f32[3,32,32,8]{2,3,1,0:T(8,128)} %copy.11), channel_id=1, source_target_pairs={{0,2},{2,0},{1,3},{3,1},{4,6},{6,4},{5,7},{7,5},{8,10},{10,8},{9,1... | collective-permute-start | bytes 294920 | tf_op jit(solution)/shard_map/ppermute | solution.py:18
  67.5 41.3 %collective-permute-start.3 = (f32[3,32,32,8]{2,3,1,0:T(8,128)S(1)}, f32[3,32,32,8]{2,3,1,0:T(8,128)}, u32[]{:S(2)}, u32[]{:S(2)}) collective-permute-start(f32[3,32,32,8]{2,3,1,0:T(8,128)S(1)} %copy.12), channel_id=1, source_target_pairs={{2,0},{0,2},{3,1},{1,3},{6,4},{4,6},{7,5},{5,7},{10,8},{8,10},{11,... | collective-permute-start | bytes 294920 | tf_op jit(solution)/shard_map/ppermute | solution.py:21
  131.0 1.7 %copy-start = (f32[3,64,16,128]{3,2,1,0:T(8,128)S(1)}, f32[3,64,16,128]{3,2,1,0:T(8,128)}, u32[]{:S(2)}) copy-start(f32[3,64,16,128]{3,2,1,0:T(8,128)} %all-gather.2.cloned.1.call-done) | copy-start | bytes 4718596
Sparse Core Ops, SparseCore 0:
  123.9 7.0 all-gather.1
where the time goes:
time: 148 us; the launch traced here: 147 us
  blocking collectives  73.7 us (50%)
  other arithmetic  25.8 us (17%)
  waiting for transfers between devices  18.9 us (13%)
  between operations  16.3 us (11%)
  local copies, waits for them, and re-layouts  6.76 us (5%)
  starting transfers between devices  5.97 us (4%)
    pmax x1, blocking collectives, local(): peak = lax.pmax(local_peak, ('tile', 'row', 'lev'))  38 us
    psum x1, blocking collectives, local(): lax.psum((base_mass, raised_mass), ('tile', 'row', 'lev'))  35.6 us
    ppermute x2, waiting for transfers between devices, padded(): lax.ppermute(lax.slice_in_dim(block, block.shape[dim] - width, None, axis...  9.37 us
    all_gather x1, waiting for transfers between devices, local(): columns = lax.all_gather(state, 'lev', axis=1, tiled=True)  7.22 us
    mul x4, other arithmetic, advance(): flux_east = centre * zonal_new  6 us
    ppermute x2, starting transfers between devices, padded(): lax.ppermute(lax.slice_in_dim(block, 0, width, axis=dim), axis, backward)  5.87 us
    reduce_sum x2, other arithmetic, remap_columns(): merid_sum = merid_sum + jnp.sum(merid[lower:upper, None] * over, 0)  5.59 us
    sub x3, other arithmetic, advance(): centre[:, 1:-1, 1:-1]  2.99 us
  transfers between devices with their start and end apart: 5, of which 3 were waited for; matrix products, arithmetic and copies ran while one was open for 1% of the time, Pallas kernels for 0%

commit v1 on v0

v1 whole, which is shorter than its diff:
```python
import jax
import jax.numpy as jnp
from jax import lax
from jax.experimental import pallas as pl
from jax.experimental.pallas import tpu as pltpu
from jax.sharding import PartitionSpec as P

NSUB = 4
CFL_NUMBER = 0.8
RIM = 2 * NSUB
SUB = 8
MESH = pl.DeviceIdType.MESH


def make_kernel(T, R, V, L, X, Y):
    NB = X // SUB
    LG = L // SUB
    XP = X + 2 * RIM
    sides = (1,) if R == 2 else (1, R - 1)
    NS = len(sides)
    WIN = 2 * RIM
    offsets = set()
    for d in range(1, T):
        offsets.add((d, 0, 0))
    for r in range(R):
        for v in range(V):
            offsets.add((0, r, v))
    for r in (1, R - 1):
        for t in (1, T - 1):
            offsets.add((t, r, 0))
    offsets.discard((0, 0, 0))
    offsets = sorted(offsets)
    group = [(r, v) for r in range(R) for v in range(V)]
    peers = [p for p in group if p != (0, 0)]
    levels = V * L
    marks = L + 1
    block = 11 if marks % 11 == 0 else marks

    def kernel(t_ref, z_ref, m_ref, c_ref, th_ref, zo_ref, mo_ref,
               bump, pack, rim_pack, rim, rim_codes, part1, part2, fin, tops,
               s_part1, r_part1, s_part2, r_part2, s_row, r_row, s_cor, r_cor,
               s_rim, r_rim, s_code, r_code, s_lev, r_lev):
        me_t = lax.axis_index("tile")
        me_r = lax.axis_index("row")
        me_v = lax.axis_index("lev")

        def dev(dt, dr, dv):
            return {
                "tile": lax.rem(me_t + dt, T),
                "row": lax.rem(me_r + dr, R),
                "lev": lax.rem(me_v + dv, V),
            }

        def remote(src, dst, send, recv, where):
            return pltpu.make_async_remote_copy(
                src_ref=src, dst_ref=dst, send_sem=send, recv_sem=recv,
                device_id=where, device_id_type=MESH)

        barrier = pltpu.get_barrier_semaphore()
        for o in offsets:
            pl.semaphore_signal(barrier, inc=1, device_id=dev(*o), device_id_type=MESH)

        lane = lax.broadcasted_iota(jnp.int32, (SUB, Y), 1)
        sub = lax.broadcasted_iota(jnp.int32, (SUB, Y), 0)
        fields = (t_ref, z_ref, m_ref)
        flat = [f.reshape(L * X, Y) for f in fields]

        def bump_of(codes):
            return 2.0 * (codes & 4095).astype(jnp.float32) / 4095.0

        base = jnp.zeros((SUB, Y), jnp.float32)
        risen = jnp.zeros((SUB, Y), jnp.float32)
        top = jnp.full((SUB, Y), -jnp.inf, jnp.float32)
        for b in range(NB):
            here = bump_of(c_ref[b * SUB:(b + 1) * SUB, :])
            bump[RIM + b * SUB:RIM + (b + 1) * SUB, :] = here
            for k in range(L):
                t = t_ref[k, b * SUB:(b + 1) * SUB, :]
                up = t + here
                base = base + t
                risen = risen + up
                top = jnp.maximum(top, up)
        base = jnp.sum(base, 0, keepdims=True)
        risen = jnp.sum(risen, 0, keepdims=True)
        top = jnp.max(top, 0, keepdims=True)
        mine = jnp.where(sub == 0, base, jnp.where(sub == 1, risen, top))
        part1[me_t] = mine

        def combine(a, b):
            return jnp.where(sub < 2, a + b, jnp.maximum(a, b))

        def pack_chunk(lg, carry):
            for b in range(NB):
                for f in range(3):
                    acc = jnp.zeros((SUB, Y), jnp.float32)
                    for g in range(SUB):
                        x = b * SUB + g
                        s = flat[f][pl.ds(lg * SUB * X + x, SUB, stride=X), :]
                        if f == 0:
                            s = s + bump[RIM + x:RIM + x + 1, :]
                        s = pltpu.roll(s, (RIM + WIN * g) % Y, 1)
                        acc = jnp.where(lane // WIN == g, s, acc)
                    pack[b, lg, f] = acc
            return carry

        lax.fori_loop(0, LG, pack_chunk, 0)
        pl.semaphore_wait(barrier, len(offsets))

        part1_copies = []
        for d in range(1, T):
            c = remote(part1.at[me_t], part1.at[me_t], s_part1.at[d - 1], r_part1.at[d - 1], dev(d, 0, 0))
            c.start()
            part1_copies.append(c)
        code_copies = [
            remote(c_ref.at[pl.ds(X - RIM, RIM)], rim_codes.at[0], s_code.at[0], r_code.at[0], dev(1, 0, 0)),
            remote(c_ref.at[pl.ds(0, RIM)], rim_codes.at[1], s_code.at[1], r_code.at[1], dev(T - 1, 0, 0)),
        ]
        for c in code_copies:
            c.start()
        pack_copies = []
        for n, dr in enumerate(sides):
            pack_copies.append(remote(pack.at[NB - 1], rim_pack.at[n, 0], s_cor.at[n, 0], r_cor.at[n, 0], dev(1, dr, 0)))
            pack_copies.append(remote(pack.at[0], rim_pack.at[n, NB + 1], s_cor.at[n, 1], r_cor.at[n, 1], dev(T - 1, dr, 0)))
            pack_copies.append(remote(pack, rim_pack.at[n, pl.ds(1, NB)], s_row.at[n], r_row.at[n], dev(0, dr, 0)))
        for c in pack_copies:
            c.start()

        def rim_copies(lg):
            out = []
            for f in range(3):
                for way, first, dt in ((0, X - RIM, 1), (1, 0, T - 1)):
                    out.append(remote(
                        fields[f].at[pl.ds(lg * SUB, SUB), pl.ds(first, RIM)],
                        rim.at[way, lg, f], s_rim.at[way, lg, f], r_rim.at[way, lg, f],
                        dev(dt, 0, 0)))
            return out

        for lg in range(LG):
            for c in rim_copies(lg):
                c.start()

        for c in part1_copies:
            c.wait()
        total = part1[0]
        for d in range(1, T):
            total = combine(total, part1[d])
        slot = me_r * V + me_v
        part2[slot] = total
        part2_copies = []
        for n, (r, v) in enumerate(peers):
            c = remote(part2.at[slot], part2.at[slot], s_part2.at[n], r_part2.at[n], dev(0, r, v))
            c.start()
            part2_copies.append(c)
        for c in code_copies:
            c.wait()
        bump[0:RIM, :] = bump_of(rim_codes[0])
        bump[RIM + X:XP, :] = bump_of(rim_codes[1])
        for c in part2_copies:
            c.wait()
        total = part2[0]
        for n in range(1, R * V):
            total = combine(total, part2[n])
        base_all = jnp.sum(total[0:1, :], 1, keepdims=True)
        risen_all = jnp.sum(total[1:2, :], 1, keepdims=True)
        peak = jnp.max(total[2:3, :], 1, keepdims=True)
        factor = base_all / risen_all
        half = 0.5 * CFL_NUMBER / jnp.sqrt(peak)
        factor = jnp.broadcast_to(factor, (SUB, 2 * Y))
        half = jnp.broadcast_to(half, (SUB, 2 * Y))
        for c in pack_copies:
            c.wait()

        def lev_copies(lg):
            place = fin.at[me_v * LG + lg]
            return [
                remote(place, place, s_lev.at[v - 1, lg], r_lev.at[v - 1, lg], dev(0, 0, v))
                for v in range(1, V)
            ]

        def chunk(lg, carry):
            for c in rim_copies(lg):
                c.wait()
            low = [rim.at[0, lg, f].reshape(SUB * RIM, Y) for f in range(3)]
            high = [rim.at[1, lg, f].reshape(SUB * RIM, Y) for f in range(3)]

            def load(f, i):
                if i < RIM:
                    main = low[f][pl.ds(i, SUB, stride=RIM), :]
                elif i < RIM + X:
                    main = flat[f][pl.ds(lg * SUB * X + i - RIM, SUB, stride=X), :]
                else:
                    main = high[f][pl.ds(i - RIM - X, SUB, stride=RIM), :]
                if f == 0:
                    main = main + bump[i:i + 1, :]
                b, g = i // SUB, i % SUB
                shift = (2 * Y - RIM - WIN * g) % Y
                wing = pltpu.roll(rim_pack[0, b, lg, f], shift, 1)
                if NS == 2:
                    other = pltpu.roll(rim_pack[1, b, lg, f], shift, 1)
                    wing = jnp.where(lane < Y // 2, other, wing)
                both = jnp.concatenate([main, wing], 1)
                return both * factor if f == 0 else both

            memo = {}

            def keep(key, make):
                if key not in memo:
                    memo[key] = make()
                return memo[key]

            def ddy(a):
                return pltpu.roll(a, 2 * Y - 1, 1) - pltpu.roll(a, 1, 1)

            def H(s, i):
                if s == 0:
                    return keep(("h", 0, i), lambda: load(0, i))
                return keep(("h", s, i), lambda: H(s - 1, i) - half * (
                    (FE(s, i + 1) - FE(s, i - 1)) + ddy(H(s - 1, i) * W2(s, i))))

            def W1(s, i):
                if s == 0:
                    return keep(("u", 0, i), lambda: load(1, i))
                return keep(("u", s, i), lambda: W1(s - 1, i) - half * (H(s - 1, i + 1) - H(s - 1, i - 1)))

            def W2(s, i):
                if s == 0:
                    return keep(("v", 0, i), lambda: load(2, i))
                return keep(("v", s, i), lambda: W2(s - 1, i) - half * ddy(H(s - 1, i)))

            def FE(s, i):
                return keep(("e", s, i), lambda: H(s - 1, i) * W1(s, i))

            mine_at = me_v * LG + lg
            for x in range(X):
                i = x + RIM
                fin[mine_at, 0, pl.ds(x, SUB, stride=X), :] = H(NSUB, i)[:, :Y]
                fin[mine_at, 1, pl.ds(x, SUB, stride=X), :] = W1(NSUB, i)[:, :Y]
                fin[mine_at, 2, pl.ds(x, SUB, stride=X), :] = W2(NSUB, i)[:, :Y]
            for c in lev_copies(lg):
                c.start()
            return carry

        lax.fori_loop(0, LG, chunk, 0)
        for lg in range(LG):
            for c in lev_copies(lg):
                c.wait()

        first = me_v * L
        for b in range(NB):
            rows = slice(b * SUB, (b + 1) * SUB)

            def prefix(c, run):
                for j in range(SUB):
                    tops[c * SUB + j] = run
                    run = run + fin[c, 0, j * X + b * SUB:j * X + (b + 1) * SUB, :]
                return run

            total = lax.fori_loop(0, V * LG, prefix, jnp.zeros((SUB, Y), jnp.float32))
            layer = total / levels
            last = None
            for start in range(0, marks, block):
                goals = [
                    total * ((first + start + n).astype(jnp.float32) / levels)
                    for n in range(block)
                ]

                def gather(c, sums):
                    sums = list(sums)
                    for j in range(SUB):
                        at = slice(j * X + b * SUB, j * X + (b + 1) * SUB)
                        h = fin[c, 0, at, :]
                        z = fin[c, 1, at, :]
                        m = fin[c, 2, at, :]
                        t = tops[c * SUB + j]
                        for n in range(block):
                            over = jnp.minimum(jnp.maximum(goals[n] - t, 0.0), h)
                            sums[2 * n] = sums[2 * n] + z * over
                            sums[2 * n + 1] = sums[2 * n + 1] + m * over
                    return tuple(sums)

                zero = jnp.zeros((SUB, Y), jnp.float32)
                sums = lax.fori_loop(0, V * LG, gather, (zero,) * (2 * block))
                for n in range(block):
                    now = (sums[2 * n], sums[2 * n + 1])
                    if last is not None:
                        k = start + n - 1
                        th_ref[k, rows, :] = layer
                        zo_ref[k, rows, :] = (now[0] - last[0]) / layer
                        mo_ref[k, rows, :] = (now[1] - last[1]) / layer
                    last = now

    vm = lambda *s: pltpu.VMEM(s, jnp.float32)
    dma = lambda *s: pltpu.SemaphoreType.DMA(s)
    scratch = [
        vm(XP, Y),
        vm(NB, LG, 3, SUB, Y),
        vm(NS, NB + 2, LG, 3, SUB, Y),
        vm(2, LG, 3, SUB, RIM, Y),
        pltpu.VMEM((2, RIM, Y), jnp.int32),
        vm(T, SUB, Y),
        vm(R * V, SUB, Y),
        vm(V * LG, 3, SUB * X, Y),
        vm(levels, SUB, Y),
        dma(T - 1), dma(T - 1), dma(R * V - 1), dma(R * V - 1),
        dma(NS), dma(NS), dma(NS, 2), dma(NS, 2),
        dma(2, LG, 3), dma(2, LG, 3), dma(2), dma(2),
        dma(V - 1, LG), dma(V - 1, LG),
    ]
    return kernel, scratch


def solution(mesh):
    T, R, V = mesh.shape["tile"], mesh.shape["row"], mesh.shape["lev"]

    def local(thickness, zonal_wind, merid_wind, pert_codes):
        L, X, Y = thickness.shape
        kernel, scratch = make_kernel(T, R, V, L, X, Y)
        spec = pl.BlockSpec(memory_space=pltpu.VMEM)
        out = jax.ShapeDtypeStruct((L, X, Y), jnp.float32)
        return pl.pallas_call(
            kernel,
            out_shape=(out,) * 3,
            in_specs=[spec] * 4,
            out_specs=(spec,) * 3,
            scratch_shapes=scratch,
            compiler_params=pltpu.CompilerParams(collective_id=0, has_side_effects=True),
        )(thickness, zonal_wind, merid_wind, pert_codes)

    field = P(("member", "lev"), "tile", "row")
    return jax.shard_map(
        local, mesh=mesh,
        in_specs=(field, field, field, P(("member", "tile"), "row")),
        out_specs=(field,) * 3, check_vma=False)
```

time: 148 us -> 41.6 us (0.28)
  blocking collectives: 73.7 us -> 0 us
  Pallas kernels: 0 us -> 37.3 us
  other arithmetic: 25.8 us -> 0 us
  waiting for transfers between devices: 18.9 us -> 0 us
  between operations: 16.3 us -> 0.65 us
  starting transfers between devices: 5.97 us -> 0 us
  local copies, waits for them, and re-layouts: 6.76 us -> 3.46 us
    pmax x1 -> x0, blocking collectives: 38 us -> none  [local(): peak = lax.pmax(local_peak, ('tile', 'row', 'lev'))]
    pallas_call x0 -> x1, Pallas kernels: none -> 37.3 us  [local(): pl.pallas_call(kernel, out_shape=(out,) * 3, in_specs=[spec] * 4, out_spe...]
    psum x1 -> x0, blocking collectives: 35.6 us -> none  [local(): lax.psum((base_mass, raised_mass), ('tile', 'row', 'lev'))]
    ppermute x4 -> x0, waiting for transfers between devices: 11.7 us -> none  [the longest x2 9.37 us: padded(): lax.ppermute(lax.slice_in_dim(block, block.shape[dim] - width, None, axis...]
    all_gather x1 -> x0, waiting for transfers between devices: 7.22 us -> none  [local(): columns = lax.all_gather(state, 'lev', axis=1, tiled=True)]
    mul x5 -> x0, other arithmetic: 6.09 us -> none  [the longest x4 6 us: advance(): flux_east = centre * zonal_new]
    ppermute x4 -> x0, starting transfers between devices: 5.93 us -> none  [the longest x2 5.87 us: padded(): lax.ppermute(lax.slice_in_dim(block, 0, width, axis=dim), axis, backward)]
    reduce_sum x3 -> x0, other arithmetic: 5.66 us -> none  [the longest x2 5.59 us: remap_columns(): merid_sum = merid_sum + jnp.sum(merid[lower:upper, None] * over, 0)]
  transfers between devices with their start and end apart: 5 -> 0, of which waited for: 3 -> 0; matrix products, arithmetic and copies ran while one was open for 1% -> 0% of each run, Pallas kernels for 0% -> 0%
where the time goes in v1:
time: 41.6 us; the launch traced here: 41.4 us
  Pallas kernels  37.3 us (90%)
  local copies, waits for them, and re-layouts  3.46 us (8%)
  between operations  0.65 us (2%)
    pallas_call x1, Pallas kernels, local(): pl.pallas_call(kernel, out_shape=(out,) * 3, in_specs=[spec] * 4, out_spe...  37.3 us
    unnamed x7, local copies, waits for them, and re-layouts  3.46 us

profile of v1, /device:TPU:0, one launch (start us, length us, event | category | flops | bytes accessed | tf_op | source)
XLA Modules:
  0.0 41.4 jit_solution(12630844569673510558)
XLA Ops:
  0.6 37.3 %shard_map.67 = (f32[32,16,128]{2,1,0:T(8,128)}, f32[32,16,128]{2,1,0:T(8,128)}, f32[32,16,128]{2,1,0:T(8,128)}) custom-call(f32[32,16,128]{2,1,0:T(8,128)} %t_ref.1, f32[32,16,128]{2,1,0:T(8,128)} %z_ref.1, f32[32,16,128]{2,1,0:T(8,128)} %m_ref.1, s32[16,128]{1,0:T(8,128)} %c_ref.1), custom_call_target="tpu_custom_call" | custom-call | tf_op jit(solution)/shard_map/pallas_call | solution.py:320
  38.0 0.0 copy-start.1
  38.0 1.7 %copy.10 = f32[32,16,128]{2,1,0:T(8,128)} copy(f32[32,16,128]{2,1,0:T(8,128)} %get-tuple-element.6) | data formatting | bytes 524288
  39.7 0.0 copy-done.1
  39.7 0.0 copy-start
  39.7 0.7 %copy.11 = f32[32,16,128]{2,1,0:T(8,128)} copy(f32[32,16,128]{2,1,0:T(8,128)S(1)} %copy-done.1) | data formatting | bytes 524288
  40.4 0.3 copy-done
  40.7 0.7 %copy.12 = f32[32,16,128]{2,1,0:T(8,128)} copy(f32[32,16,128]{2,1,0:T(8,128)S(1)} %copy-done) | data formatting | bytes 524288
Async XLA Ops:
  38.0 1.7 %copy-start.1 = (f32[32,16,128]{2,1,0:T(8,128)S(1)}, f32[32,16,128]{2,1,0:T(8,128)}, u32[]{:S(2)}) copy-start(f32[32,16,128]{2,1,0:T(8,128)} %get-tuple-element.7) | copy-start | bytes 786436
  39.7 1.0 %copy-start = (f32[32,16,128]{2,1,0:T(8,128)S(1)}, f32[32,16,128]{2,1,0:T(8,128)}, u32[]{:S(2)}) copy-start(f32[32,16,128]{2,1,0:T(8,128)} %get-tuple-element.8) | copy-start | bytes 786436

commit v2 on v1

--- a/solution.py
+++ b/solution.py
@@ -9,6 +9,8 @@
 CFL_NUMBER = 0.8
 RIM = 2 * NSUB
 SUB = 8
+FIRST = 1
+VMEM = 65466368
 MESH = pl.DeviceIdType.MESH
 
 
@@ -36,8 +38,8 @@
     marks = L + 1
     block = 11 if marks % 11 == 0 else marks
 
-    def kernel(t_ref, z_ref, m_ref, c_ref, th_ref, zo_ref, mo_ref,
-               bump, pack, rim_pack, rim, rim_codes, part1, part2, fin, tops,
+    def kernel(t_in, z_in, m_in, c_in, out,
+               t_ref, z_ref, m_ref, c_ref, s_in, bump, pack, rim_pack, rim, rim_codes, part1, part2, own, s_out,
                s_part1, r_part1, s_part2, r_part2, s_row, r_row, s_cor, r_cor,
                s_rim, r_rim, s_code, r_code, s_lev, r_lev):
         me_t = lax.axis_index("tile")
@@ -60,10 +62,40 @@
         for o in offsets:
             pl.semaphore_signal(barrier, inc=1, device_id=dev(*o), device_id_type=MESH)
 
+        loads = [
+            pltpu.make_async_copy(a, b, s_in.at[n])
+            for n, (a, b) in enumerate(((t_in, t_ref), (z_in, z_ref), (m_in, m_ref), (c_in, c_ref)))
+        ]
+        for c in loads:
+            c.start()
+
         lane = lax.broadcasted_iota(jnp.int32, (SUB, Y), 1)
         sub = lax.broadcasted_iota(jnp.int32, (SUB, Y), 0)
         fields = (t_ref, z_ref, m_ref)
         flat = [f.reshape(L * X, Y) for f in fields]
+
+        def rim_copies(lg):
+            out = []
+            for f in range(3):
+                for way, first, dt in ((0, X - RIM, 1), (1, 0, T - 1)):
+                    out.append(remote(
+                        fields[f].at[pl.ds(lg * SUB, SUB), pl.ds(first + (f if way == 0 else 0), RIM - f)],
+                        rim.at[way, lg, f, :, pl.ds(f if way == 0 else 0, RIM - f)], s_rim.at[way, lg, f], r_rim.at[way, lg, f],
+                        dev(dt, 0, 0)))
+            return out
+
+        for c in loads:
+            c.wait()
+        pl.semaphore_wait(barrier, len(offsets))
+        for lg in range(FIRST):
+            for c in rim_copies(lg):
+                c.start()
+        code_copies = [
+            remote(c_ref.at[pl.ds(X - RIM, RIM)], rim_codes.at[0], s_code.at[0], r_code.at[0], dev(1, 0, 0)),
+            remote(c_ref.at[pl.ds(0, RIM)], rim_codes.at[1], s_code.at[1], r_code.at[1], dev(T - 1, 0, 0)),
+        ]
+        for c in code_copies:
+            c.start()
 
         def bump_of(codes):
             return 2.0 * (codes & 4095).astype(jnp.float32) / 4095.0
@@ -89,6 +121,11 @@
         def combine(a, b):
             return jnp.where(sub < 2, a + b, jnp.maximum(a, b))
 
+        part1_copies = []
+        for d in range(1, T):
+            c = remote(part1.at[me_t], part1.at[me_t], s_part1.at[d - 1], r_part1.at[d - 1], dev(d, 0, 0))
+            c.start()
+            part1_copies.append(c)
         def pack_chunk(lg, carry):
             for b in range(NB):
                 for f in range(3):
@@ -104,19 +141,7 @@
             return carry
 
         lax.fori_loop(0, LG, pack_chunk, 0)
-        pl.semaphore_wait(barrier, len(offsets))
-
-        part1_copies = []
-        for d in range(1, T):
-            c = remote(part1.at[me_t], part1.at[me_t], s_part1.at[d - 1], r_part1.at[d - 1], dev(d, 0, 0))
-            c.start()
-            part1_copies.append(c)
-        code_copies = [
-            remote(c_ref.at[pl.ds(X - RIM, RIM)], rim_codes.at[0], s_code.at[0], r_code.at[0], dev(1, 0, 0)),
-            remote(c_ref.at[pl.ds(0, RIM)], rim_codes.at[1], s_code.at[1], r_code.at[1], dev(T - 1, 0, 0)),
-        ]
-        for c in code_copies:
-            c.start()
+
         pack_copies = []
         for n, dr in enumerate(sides):
             pack_copies.append(remote(pack.at[NB - 1], rim_pack.at[n, 0], s_cor.at[n, 0], r_cor.at[n, 0], dev(1, dr, 0)))
@@ -125,17 +150,7 @@
         for c in pack_copies:
             c.start()
 
-        def rim_copies(lg):
-            out = []
-            for f in range(3):
-                for way, first, dt in ((0, X - RIM, 1), (1, 0, T - 1)):
-                    out.append(remote(
-                        fields[f].at[pl.ds(lg * SUB, SUB), pl.ds(first, RIM)],
-                        rim.at[way, lg, f], s_rim.at[way, lg, f], r_rim.at[way, lg, f],
-                        dev(dt, 0, 0)))
-            return out
-
-        for lg in range(LG):
+        for lg in range(FIRST, LG):
             for c in rim_copies(lg):
                 c.start()
 
@@ -171,9 +186,9 @@
             c.wait()
 
         def lev_copies(lg):
-            place = fin.at[me_v * LG + lg]
-            return [
-                remote(place, place, s_lev.at[v - 1, lg], r_lev.at[v - 1, lg], dev(0, 0, v))
+            place = out.at[me_v * LG + lg]
+            return [pltpu.make_async_copy(own.at[lg], place, s_out.at[lg])] + [
+                remote(own.at[lg], place, s_lev.at[v - 1, lg], r_lev.at[v - 1, lg], dev(0, 0, v))
                 for v in range(1, V)
             ]
 
@@ -230,12 +245,11 @@
             def FE(s, i):
                 return keep(("e", s, i), lambda: H(s - 1, i) * W1(s, i))
 
-            mine_at = me_v * LG + lg
             for x in range(X):
                 i = x + RIM
-                fin[mine_at, 0, pl.ds(x, SUB, stride=X), :] = H(NSUB, i)[:, :Y]
-                fin[mine_at, 1, pl.ds(x, SUB, stride=X), :] = W1(NSUB, i)[:, :Y]
-                fin[mine_at, 2, pl.ds(x, SUB, stride=X), :] = W2(NSUB, i)[:, :Y]
+                own[lg, 0, pl.ds(x, SUB, stride=X), :] = H(NSUB, i)[:, :Y]
+                own[lg, 1, pl.ds(x, SUB, stride=X), :] = W1(NSUB, i)[:, :Y]
+                own[lg, 2, pl.ds(x, SUB, stride=X), :] = W2(NSUB, i)[:, :Y]
             for c in lev_copies(lg):
                 c.start()
             return carry
@@ -245,7 +259,15 @@
             for c in lev_copies(lg):
                 c.wait()
 
-        first = me_v * L
+    def remap(state, th_ref, zo_ref, mo_ref, fin, tops, s_in):
+        loads = [
+            pltpu.make_async_copy(state.at[:, f], fin.at[:, f], s_in.at[f])
+            for f in range(3)
+        ]
+        for c in loads:
+            c.start()
+        loads[0].wait()
+        first = lax.axis_index("lev") * L
         for b in range(NB):
             rows = slice(b * SUB, (b + 1) * SUB)
 
@@ -257,6 +279,9 @@
 
             total = lax.fori_loop(0, V * LG, prefix, jnp.zeros((SUB, Y), jnp.float32))
             layer = total / levels
+            if b == 0:
+                loads[1].wait()
+                loads[2].wait()
             last = None
             for start in range(0, marks, block):
                 goals = [
@@ -292,6 +317,9 @@
     vm = lambda *s: pltpu.VMEM(s, jnp.float32)
     dma = lambda *s: pltpu.SemaphoreType.DMA(s)
     scratch = [
+        vm(L, X, Y), vm(L, X, Y), vm(L, X, Y),
+        pltpu.VMEM((X, Y), jnp.int32),
+        dma(4),
         vm(XP, Y),
         vm(NB, LG, 3, SUB, Y),
         vm(NS, NB + 2, LG, 3, SUB, Y),
@@ -299,14 +327,13 @@
         pltpu.VMEM((2, RIM, Y), jnp.int32),
         vm(T, SUB, Y),
         vm(R * V, SUB, Y),
-        vm(V * LG, 3, SUB * X, Y),
-        vm(levels, SUB, Y),
+        vm(LG, 3, SUB * X, Y), dma(LG),
         dma(T - 1), dma(T - 1), dma(R * V - 1), dma(R * V - 1),
         dma(NS), dma(NS), dma(NS, 2), dma(NS, 2),
         dma(2, LG, 3), dma(2, LG, 3), dma(2), dma(2),
         dma(V - 1, LG), dma(V - 1, LG),
     ]
-    return kernel, scratch
+    return kernel, scratch, (V * LG, 3, SUB * X, Y), remap, [vm(V * LG, 3, SUB * X, Y), vm(levels, SUB, Y), dma(3)]
 
 
 def solution(mesh):
@@ -314,17 +341,26 @@
 
     def local(thickness, zonal_wind, merid_wind, pert_codes):
         L, X, Y = thickness.shape
-        kernel, scratch = make_kernel(T, R, V, L, X, Y)
+        kernel, scratch, state, remap, held = make_kernel(T, R, V, L, X, Y)
         spec = pl.BlockSpec(memory_space=pltpu.VMEM)
         out = jax.ShapeDtypeStruct((L, X, Y), jnp.float32)
+        columns = pl.pallas_call(
+            kernel,
+            out_shape=jax.ShapeDtypeStruct(state, jnp.float32),
+            in_specs=[pl.BlockSpec(memory_space=pl.ANY)] * 4,
+            out_specs=pl.BlockSpec(memory_space=pl.ANY),
+            scratch_shapes=scratch,
+            compiler_params=pltpu.CompilerParams(
+                collective_id=0, has_side_effects=True, vmem_limit_bytes=VMEM),
+        )(thickness, zonal_wind, merid_wind, pert_codes)
         return pl.pallas_call(
-            kernel,
+            remap,
             out_shape=(out,) * 3,
-            in_specs=[spec] * 4,
+            in_specs=[pl.BlockSpec(memory_space=pl.ANY)],
             out_specs=(spec,) * 3,
-            scratch_shapes=scratch,
-            compiler_params=pltpu.CompilerParams(collective_id=0, has_side_effects=True),
-        )(thickness, zonal_wind, merid_wind, pert_codes)
+            scratch_shapes=held,
+            compiler_params=pltpu.CompilerParams(vmem_limit_bytes=VMEM),
+        )(columns)
 
     field = P(("member", "lev"), "tile", "row")
     return jax.shard_map(

time: 41.6 us -> 36.6 us (0.88)
  local copies, waits for them, and re-layouts: 3.46 us -> 0 us
  Pallas kernels: 37.3 us -> 35.7 us
    unnamed x7 -> x0, local copies, waits for them, and re-layouts: 3.46 us -> none
    pallas_call x1 -> x2, Pallas kernels: 37.3 us -> 35.7 us  [the longest x1 29.1 us: local(): pl.pallas_call(kernel, out_shape=jax.ShapeDtypeStruct(state, jnp.float32)...]
where the time goes in v2:
time: 36.6 us; the launch traced here: 36.4 us
  Pallas kernels  35.7 us (98%)
  between operations  0.64 us (2%)
    pallas_call x1, Pallas kernels, local(): pl.pallas_call(kernel, out_shape=jax.ShapeDtypeStruct(state, jnp.float32)...  29.1 us
    pallas_call x1, Pallas kernels, local(): pl.pallas_call(remap, out_shape=(out,) * 3, in_specs=[pl.BlockSpec(memory...  6.7 us

profile of v2, /device:TPU:0, one launch (start us, length us, event | category | flops | bytes accessed | tf_op | source)
XLA Modules:
  0.0 36.4 jit_solution(12065435689547795073)
XLA Ops:
  0.6 29.1 %shard_map.67.state = f32[8,3,128,128]{3,2,1,0:T(8,128)} custom-call(f32[32,16,128]{2,1,0:T(8,128)} %t_in.1, f32[32,16,128]{2,1,0:T(8,128)} %z_in.1, f32[32,16,128]{2,1,0:T(8,128)} %m_in.1, s32[16,128]{1,0:T(8,128)} %c_in.1), custom_call_target="tpu_custom_call" | custom-call | tf_op jit(solution)/shard_map/pallas_call | solution.py:347
  29.7 6.7 %shard_map.68 = (f32[32,16,128]{2,1,0:T(8,128)}, f32[32,16,128]{2,1,0:T(8,128)}, f32[32,16,128]{2,1,0:T(8,128)}) custom-call(f32[8,3,128,128]{3,2,1,0:T(8,128)} %shard_map.67.state), custom_call_target="tpu_custom_call" | custom-call | tf_op jit(solution)/shard_map/pallas_call | solution.py:356

commit v3 on v2

--- a/solution.py
+++ b/solution.py
@@ -259,7 +259,15 @@
             for c in lev_copies(lg):
                 c.wait()
 
-    def remap(state, th_ref, zo_ref, mo_ref, fin, tops, s_in):
+    def remap(state, th_out, zo_out, mo_out, fin, tops, s_in, th_ref, zo_ref, mo_ref, s_done):
+        stores = []
+
+        def store(n, b, src, dst):
+            at = (slice(None), pl.ds(b * SUB, SUB))
+            c = pltpu.make_async_copy(src.at[at], dst.at[at], s_done.at[n, b])
+            c.start()
+            stores.append(c)
+
         loads = [
             pltpu.make_async_copy(state.at[:, f], fin.at[:, f], s_in.at[f])
             for f in range(3)
@@ -282,6 +290,9 @@
             if b == 0:
                 loads[1].wait()
                 loads[2].wait()
+            for k in range(L):
+                th_ref[k, rows, :] = layer
+            store(0, b, th_ref, th_out)
             last = None
             for start in range(0, marks, block):
                 goals = [
@@ -309,10 +320,13 @@
                     now = (sums[2 * n], sums[2 * n + 1])
                     if last is not None:
                         k = start + n - 1
-                        th_ref[k, rows, :] = layer
                         zo_ref[k, rows, :] = (now[0] - last[0]) / layer
                         mo_ref[k, rows, :] = (now[1] - last[1]) / layer
                     last = now
+            store(1, b, zo_ref, zo_out)
+            store(2, b, mo_ref, mo_out)
+        for c in stores:
+            c.wait()
 
     vm = lambda *s: pltpu.VMEM(s, jnp.float32)
     dma = lambda *s: pltpu.SemaphoreType.DMA(s)
@@ -333,7 +347,7 @@
         dma(2, LG, 3), dma(2, LG, 3), dma(2), dma(2),
         dma(V - 1, LG), dma(V - 1, LG),
     ]
-    return kernel, scratch, (V * LG, 3, SUB * X, Y), remap, [vm(V * LG, 3, SUB * X, Y), vm(levels, SUB, Y), dma(3)]
+    return kernel, scratch, (V * LG, 3, SUB * X, Y), remap, [vm(V * LG, 3, SUB * X, Y), vm(levels, SUB, Y), dma(3), vm(L, X, Y), vm(L, X, Y), vm(L, X, Y), dma(3, NB)]
 
 
 def solution(mesh):
@@ -342,7 +356,6 @@
     def local(thickness, zonal_wind, merid_wind, pert_codes):
         L, X, Y = thickness.shape
         kernel, scratch, state, remap, held = make_kernel(T, R, V, L, X, Y)
-        spec = pl.BlockSpec(memory_space=pltpu.VMEM)
         out = jax.ShapeDtypeStruct((L, X, Y), jnp.float32)
         columns = pl.pallas_call(
             kernel,
@@ -357,7 +370,7 @@
             remap,
             out_shape=(out,) * 3,
             in_specs=[pl.BlockSpec(memory_space=pl.ANY)],
-            out_specs=(spec,) * 3,
+            out_specs=(pl.BlockSpec(memory_space=pl.ANY),) * 3,
             scratch_shapes=held,
             compiler_params=pltpu.CompilerParams(vmem_limit_bytes=VMEM),
         )(columns)

time: 36.6 us -> 36.4 us (level)
  no operation moved by 1% of the time
where the time goes in v3:
time: 36.4 us; the launch traced here: 36.3 us
  Pallas kernels  35.6 us (98%)
  between operations  0.64 us (2%)
    pallas_call x1, Pallas kernels, local(): pl.pallas_call(kernel, out_shape=jax.ShapeDtypeStruct(state, jnp.float32)...  29.1 us
    pallas_call x1, Pallas kernels, local(): pl.pallas_call(remap, out_shape=(out,) * 3, in_specs=[pl.BlockSpec(memory...  6.56 us

profile of v3, /device:TPU:0, one launch (start us, length us, event | category | flops | bytes accessed | tf_op | source)
XLA Modules:
  0.0 36.3 jit_solution(7227339930409299513)
XLA Ops:
  0.6 29.1 %shard_map.67.state = f32[8,3,128,128]{3,2,1,0:T(8,128)} custom-call(f32[32,16,128]{2,1,0:T(8,128)} %t_in.1, f32[32,16,128]{2,1,0:T(8,128)} %z_in.1, f32[32,16,128]{2,1,0:T(8,128)} %m_in.1, s32[16,128]{1,0:T(8,128)} %c_in.1), custom_call_target="tpu_custom_call" | custom-call | tf_op jit(solution)/shard_map/pallas_call | solution.py:360
  29.7 6.6 %shard_map.68 = (f32[32,16,128]{2,1,0:T(8,128)}, f32[32,16,128]{2,1,0:T(8,128)}, f32[32,16,128]{2,1,0:T(8,128)}) custom-call(f32[8,3,128,128]{3,2,1,0:T(8,128)} %shard_map.67.state), custom_call_target="tpu_custom_call" | custom-call | tf_op jit(solution)/shard_map/pallas_call | solution.py:369
